TPU v7x, 128 devices: a whole 4x4x4 slice. The times are simulated.
128 devices in a mesh: row: 8 (over x, core), col: 16 (over z, y).
Axes of the slice: x: 4, y: 4, z: 4, core: 2. Of those that a mesh axis runs over, the one named last changes fastest.
Arguments:
- coords: float32 [3, 2097152], P(None, ('row', 'col')), may hold values from 0 to 6
- vectors: bfloat16 [64, 2097152], P(None, ('row', 'col')), may hold values from -0.59765625 to 0.59765625
- basis: bfloat16 [32, 2097152], P(None, ('row', 'col')), may hold values from -1.5 to 1.5
- transfer: float32 [32, 262144], P(None, ('row', 'col')), may hold values from -0.3 to 0.3
- leaf_skeleton: float32 [3, 262144], P(None, ('row', 'col')), may hold values from 0 to 6
- device_skeleton: float32 [3, 4096], P(None, ('row', 'col')), may hold values from 0 to 6
- near_pairs: int32 [2, 49152], P(None, ('row', 'col')), may hold values from 0 to 8191, as said below
- far_leaves: int32 [8192, 8], P(('row', 'col')), may hold values from 0 to 8191, as said below
- far_devices: int32 [128, 16], P(('row', 'col')), may hold values from 0 to 127
Outputs:
- product: float32 [64, 2097152], P(None, ('row', 'col'))
Inputs may be any that keep to these rules, and one draw needn't show every extreme that they name: `near_pairs`: device k of the row x col grid (k = row index * 16 + col index) holds near blocks k * 6 * 64 to (k + 1) * 6 * 64 - 1 and leaves k * 64 to (k + 1) * 64 - 1; the target and the source leaf of each of its near blocks lie on device k or on a device beside it in the grid, diagonals included. `far_leaves`: the coupling partners of a leaf lie on that leaf's device or on a device beside it in the row x col grid, diagonals included.
All inputs are finite; a program needn't handle non-finite values.
Results may differ from a plain program's by a relative error of at most 0.004.
Values may be sent and summed in bfloat16 or wider, within the bound.
A program may use at most 256 MiB of HBM per device.

v0:
```python
import math
import jax
import jax.numpy as jnp
from jax import lax
from jax.sharding import PartitionSpec as P

HIGH = lax.Precision.HIGHEST


def with_halo(array, sides, width):
    for axis, dim in sides:
        devices, length = (lax.axis_size(axis), array.shape[dim])
        up = [(i, (i + 1) % devices) for i in range(devices - 1)]
        down = [(j, i) for i, j in up]
        last = lax.slice_in_dim(array, length - width, length, axis=dim)
        initial = lax.slice_in_dim(array, 0, width, axis=dim)
        before = lax.ppermute(last, axis, up)
        after = lax.ppermute(initial, axis, down)
        array = jnp.concatenate([before, array, after], axis=dim)
    return array


def from_behind(block, axis, distance):
    devices = range(lax.axis_size(axis))
    route = [(i - distance, i) for i in devices if i - distance in devices]
    return lax.ppermute(block, axis, route)


def turned_gather(arrays, axis, dims):
    turned = [jnp.moveaxis(a, dim, 0) for a, dim in zip(arrays, dims)]
    both = jnp.concatenate([t.reshape(len(t), -1) for t in turned], axis=1)
    result, at, outs = (lax.all_gather(both, axis, axis=0, tiled=True), 0, [])
    for t, dim in zip(turned, dims):
        share = result[:, at : at + t[0].size].reshape(-1, *t.shape[1:])
        outs.append(jnp.moveaxis(share, 0, dim))
        at += t[0].size
    return tuple(outs)


def kernel_block(left, right):
    total = None
    for dimension in range(3):
        gap = left[..., dimension, :, None] - right[..., dimension, None, :]
        total = gap * gap if total is None else total + gap * gap
    return jnp.exp(-0.5 * total)


def upsweep(vector_rows, basis_rows):
    return jnp.einsum(
        "nvil,nril->nvir", vector_rows, basis_rows, preferred_element_type=jnp.float32
    ).astype(jnp.bfloat16)


def shards(
    coords,
    vectors,
    basis,
    transfer,
    leaf_skeleton,
    device_skeleton,
    near_pairs,
    far_leaves,
    far_devices,
):
    col_count = lax.axis_size("col")
    row_here = lax.axis_index("row")
    col_here = lax.axis_index("col")
    rank_size = basis.shape[0]
    vec_count = vectors.shape[0]
    leaves = transfer.shape[1] // rank_size
    leaf_width = coords.shape[1] // leaves
    block_group = math.gcd(near_pairs.shape[1], 32)

    def hood_of(global_leaf):
        owner_dev = global_leaf // leaves
        row_offset = owner_dev // col_count - row_here + 1
        col_offset = owner_dev % col_count - col_here + 1
        return (row_offset * 3 + col_offset, global_leaf % leaves)

    points_pad, skeleton_pad = (
        with_halo(coords[None, None], (("row", 0), ("col", 1)), 1),
        with_halo(leaf_skeleton[None, None], (("row", 0), ("col", 1)), 1),
    )
    vectors_pad, basis_pad = (
        with_halo(vectors[None, None], (("row", 0), ("col", 1)), 1),
        with_halo(basis[None, None], (("row", 0), ("col", 1)), 1),
    )
    coeff_pad = upsweep(
        vectors_pad.reshape(9, vec_count, leaves, leaf_width),
        basis_pad.reshape(9, rank_size, leaves, leaf_width),
    )
    coeff_own = coeff_pad[4]
    coords_pool = points_pad.reshape(9, 3, leaves, leaf_width)
    vectors_pool = vectors_pad.reshape(9, vec_count, leaves, leaf_width)
    tgt_hood, tgt_leaf = hood_of(near_pairs[0].reshape(-1, block_group))
    src_hood, src_leaf = hood_of(near_pairs[1].reshape(-1, block_group))

    def near_step(buffer, item):
        t_hood, t_leaf, s_hood, s_leaf = item
        tgt_points = coords_pool[t_hood, :, t_leaf, :]
        src_points = coords_pool[s_hood, :, s_leaf, :]
        block = kernel_block(tgt_points, src_points).astype(jnp.bfloat16)
        src_vectors = vectors_pool[s_hood, :, s_leaf, :]
        partial_value = jnp.einsum(
            "bvs,bts->bvt", src_vectors, block, preferred_element_type=jnp.float32
        )
        return (buffer.at[t_hood, :, t_leaf, :].add(partial_value), None)

    start = jnp.zeros((9, vec_count, leaves, leaf_width), jnp.float32)
    buffer, _ = lax.scan(near_step, start, (tgt_hood, tgt_leaf, src_hood, src_leaf))
    buffer = buffer.reshape(3, 3, vec_count, leaves * leaf_width)
    near_field = buffer[1, 1]
    for row_step in range(3):
        for col_step in range(3):
            if row_step != 1 or col_step != 1:
                offset = (row_step - 1) * col_count + (col_step - 1)
                near_field = near_field + from_behind(
                    buffer[row_step, col_step].astype(jnp.bfloat16), ("row", "col"), offset
                ).astype(jnp.float32)
    far_hood, far_leaf = hood_of(far_leaves)
    picked_coeff = coeff_pad[far_hood, :, far_leaf, :].astype(jnp.float32)
    skeleton_pool = skeleton_pad.reshape(9, 3, leaves, rank_size)
    picked_skel = skeleton_pool[far_hood, :, far_leaf, :]
    own_skel = jnp.transpose(leaf_skeleton.reshape(3, leaves, rank_size), (1, 0, 2))
    coupling = kernel_block(picked_skel, own_skel[:, None])
    leaf_far = jnp.einsum("ifvs,ifst->ivt", picked_coeff, coupling, precision=HIGH)
    transfer_mats = transfer.reshape(rank_size, leaves, rank_size)
    device_coeff = jnp.einsum(
        "vir,ris->vs", coeff_own.astype(jnp.float32), transfer_mats, precision=HIGH
    )
    all_coeffs, all_skeleton = turned_gather(
        (device_coeff, device_skeleton), ("row", "col"), (1, 1)
    )
    chosen = far_devices[0]
    top_coeffs = all_coeffs.reshape(vec_count, -1, rank_size)[:, chosen, :]
    top_skel = jnp.transpose(all_skeleton.reshape(3, -1, rank_size)[:, chosen, :], (1, 0, 2))
    coupling_top = kernel_block(top_skel, device_skeleton[None])
    device_far = jnp.einsum("vfs,fst->vt", top_coeffs, coupling_top, precision=HIGH)
    field = leaf_far + jnp.einsum("vs,ris->ivr", device_far, transfer_mats, precision=HIGH)
    field = field.astype(jnp.bfloat16)
    far_part = jnp.einsum(
        "ivr,ril->vil",
        field,
        basis.reshape(rank_size, leaves, leaf_width),
        preferred_element_type=jnp.float32,
    )
    return near_field + far_part.reshape(vec_count, leaves * leaf_width)


def solution(mesh):
    in_specs = (
        P(None, ("row", "col")),
        P(None, ("row", "col")),
        P(None, ("row", "col")),
        P(None, ("row", "col")),
        P(None, ("row", "col")),
        P(None, ("row", "col")),
        P(None, ("row", "col")),
        P(("row", "col"), None),
        P(("row", "col"), None),
    )
    out_specs = P(None, ("row", "col"))
    return jax.shard_map(shards, mesh=mesh, in_specs=in_specs, out_specs=out_specs, check_vma=False)
```

profile of v0, /device:TPU:1, one launch (start us, length us, event | category | flops | bytes accessed | tf_op | source)
XLA Modules:
  0.0 953.4 jit_solution(7944079981632862380)
XLA Ops:
  42.5 10.9 %collective-permute-done.1 = bf16[1,1,64,16384]{3,2,1,0:T(8,128)(2,1)S(1)} collective-permute-done((bf16[1,1,64,16384]{3,2,1,0:T(8,128)(2,1)}, bf16[1,1,64,16384]{3,2,1,0:T(8,128)(2,1)S(1)}, u32[]{:S(2)}, u32[]{:S(2)}) %collective-permute-start.1) | collective-permute-done | bytes 2097184 | tf_op jit(solution)/shard_map/ppermute | solution.py:18
  70.8 179.7 %collective-permute-done.7 = f32[3,1,3,16384]{3,1,2,0:T(1,128)} collective-permute-done((f32[3,1,3,16384]{3,1,2,0:T(1,128)}, f32[3,1,3,16384]{3,1,2,0:T(1,128)}, u32[]{:S(2)}, u32[]{:S(2)}) %collective-permute-start.7) | collective-permute-done | bytes 589856 | tf_op jit(solution)/shard_map/ppermute | solution.py:18
  255.0 8.6 collective-permute-done.6
  271.3 10.5 %collective-permute-start.20 = (f32[1,1,3,2048]{3,2,1,0:T(4,128)}, f32[1,1,3,2048]{3,2,1,0:T(4,128)}, u32[]{:S(2)}, u32[]{:S(2)}) collective-permute-start(f32[1,1,3,2048]{3,2,1,0:T(4,128)} %bitcast.21), channel_id=1, source_target_pairs={{0,16},{16,32},{32,48},{48,64},{64,80},{80,96},{96,112},{1,17},{17... | collective-permute-start | bytes 73736 | tf_op jit(solution)/shard_map/ppermute | solution.py:17
  281.8 7.8 pad_maximum_fusion.1
  289.6 10.5 %copy.76 = bf16[36,8,64,256]{3,2,1,0:T(8,128)(2,1)} copy(bf16[36,8,64,256]{3,1,2,0:T(8,128)(2,1)} %bitcast.197) | data formatting | bytes 18874368
  300.1 7.1 pad_maximum_fusion
  311.8 12.0 %copy.53 = bf16[9,64,64,256]{3,1,2,0:T(8,128)(2,1)} copy(bf16[9,64,64,256]{3,2,1,0:T(8,128)(2,1)S(1)} %bitcast.194) | data formatting | bytes 37748736 | tf_op jit(solution)/shard_map/while | solution.py:110
  323.8 12.6 %broadcast_in_dim.26 = f32[9,64,64,256]{3,1,2,0:T(8,128)} broadcast(f32[]{:T(128)} %constant.129.clone.1), dimensions={} | broadcast | bytes 37748740 | tf_op jit(solution)/shard_map/broadcast_in_dim | solution.py:109
  336.5 303.8 %while.10 = (s32[]{:T(128)}, f32[9,64,64,256]{3,1,2,0:T(8,128)}, s32[12,32]{1,0:T(8,128)S(1)}, s32[12,32]{1,0:T(8,128)S(1)}, s32[12,32]{1,0:T(8,128)S(1)}, /*ind...) while((s32[]{:T(128)}, f32[9,64,64,256]{3,1,2,0:T(8,128)}, ...), condition=%wide.region_2.3_spmd, body=%wide.region_0.2_spmd.sunk | while | flops 289932096 | bytes 12912617 | solution.py:110
  341.4 7.0 gather_fusion
  366.7 7.0 gather_fusion
  392.1 7.0 gather_fusion
  417.4 7.0 gather_fusion
  442.7 7.0 gather_fusion
  468.0 7.0 gather_fusion
  493.3 7.0 gather_fusion
  518.6 7.0 gather_fusion
  543.9 7.0 gather_fusion
  569.2 7.0 gather_fusion
  594.5 7.0 gather_fusion
  619.9 7.0 gather_fusion
  640.3 35.3 %copy.55 = f32[9,64,64,256]{3,2,1,0:T(8,128)} copy(f32[9,64,64,256]{3,1,2,0:T(8,128)} %get-tuple-element.47) | data formatting | bytes 75497472 | tf_op jit(solution)/shard_map/while | solution.py:110
  675.6 40.3 %reshape.193 = f32[3,3,64,16384]{3,2,1,0:T(8,128)} reshape(f32[9,64,64,256]{3,2,1,0:T(8,128)} %copy.55) | data formatting | bytes 75497472 | tf_op jit(solution)/shard_map/reshape | solution.py:111
  715.9 13.1 %convert.10 = bf16[3,3,64,16384]{3,2,1,0:T(8,128)(2,1)S(1)} convert(f32[3,3,64,16384]{3,2,1,0:T(8,128)} %reshape.193) | non-fusion elementwise | flops 9437184 | bytes 56623104 | tf_op jit(solution)/shard_map/convert.7
  744.9 28.9 %convert_bitcast_fusion = bf16[9,64,64,32]{1,3,2,0:T(8,128)(2,1)} fusion(bf16[9,32,64,256]{3,2,1,0:T(8,128)(2,1)} %bitcast.200, bf16[9,64,64,256]{3,2,1,0:T(8,128)(2,1)} %bitcast.195), kind=kOutput, calls=%fused_computation.59 | convolution fusion | flops 605159424 | bytes 30670848 | tf_op jit(solution)/shard_map/nvil,nril->nvir/dot_general | solution.py:49
  791.6 8.1 collective-permute-start.13
  801.6 7.0 collective-permute-start.11
  814.1 8.4 gather_fusion.3
  822.5 12.3 %fusion.47 = f32[64,64,32]{1,2,0:T(8,128)S(1)} fusion(bf16[64,8,64,32]{2,3,1,0:T(8,128)(2,1)} %bitcast.199, f32[64,32]{1,0:T(8,128)S(1)} %copy-done.12, f32[64,8,32]{2,1,0:T(8,128)S(1)} %bitcast.222, f32[64,32]{1,0:T(8,128)S(1)} %copy-done.13, f32[64,8,32]{2,1,0:T(8,128)S(1)} %bitcast.221, f32[64,32]{1,0:T(8,128)S(1)} %copy-done.11, ...), kind=kOutput, calls=%fused_computation.88 | convolution fusion | flops 407371776 | bytes 2842624 | tf_op jit(solution)/shard_map/ifvs,ifst->ivt/dot_general | solution.py:126
  834.8 87.4 %all-gather.2.cloned.1.call-done = f32[4096,67]{1,0:T(8,128)} async-done(((f32[32,67]{1,0:T(8,128)}), f32[4096,67]{1,0:T(8,128)}) %all-gather.2.cloned.1.call-update) | async-done | bytes 1097744 | tf_op jit(solution)/shard_map/all_gather | solution.py:32
  936.1 10.2 %fusion.37 = f32[64,16384]{1,0:T(8,128)} fusion(f32[64,16384]{1,0:T(8,128)S(1)} %bitcast.198, f32[3,3,64,16384]{3,2,1,0:T(8,128)} %reshape.193, bf16[64,16384]{1,0:T(8,128)(2,1)} %collective-permute-done.15, bf16[64,16384]{1,0:T(8,128)(2,1)} %collective-permute-done.14, bf16[64,16384]{1,0:T(8,128)(2,1)} %collective-permute-done.13, ...), kind=kLoop, calls=%fused_computation.69 | loop fusion | flops 17825792 | bytes 29360128 | tf_op jit(solution)/shard_map/add | solution.py:147
  (281 shorter events, 343.6 us)
Async XLA Ops:
  6.5 47.8 %copy-start.4 = (bf16[64,16384]{1,0:T(8,128)(2,1)S(1)}, bf16[64,16384]{1,0:T(8,128)(2,1)}, u32[]{:S(2)}) copy-start(bf16[64,16384]{1,0:T(8,128)(2,1)} %param.12) | copy-start | bytes 6291460
  6.5 915.7 %all-gather.2.cloned.1.call-start = ((), (), s32[]{:S(2)}) async-start(), calls=%async_computation | async-start | bytes 2113536 | tf_op jit(solution)/shard_map/all_gather | solution.py:32
  7.8 13.9 %collective-permute-start.4 = (f32[1,1,3,16384]{3,1,2,0:T(1,128)S(1)}, f32[1,1,3,16384]{3,1,2,0:T(1,128)S(1)}, u32[]{:S(2)}, u32[]{:S(2)}) collective-permute-start(f32[1,1,3,16384]{3,1,2,0:T(1,128)S(1)} %broadcast_in_dim.28), channel_id=1, source_target_pairs={{0,16},{16,32},{32,48},{48,64},{64,80},{80,96},{96,112},{1,17},{17... | collective-permute-start | bytes 589832 | tf_op jit(solution)/shard_map/ppermute | solution.py:17
  12.3 53.4 %collective-permute-start.5 = (f32[1,1,3,16384]{3,1,2,0:T(1,128)S(1)}, f32[1,1,3,16384]{3,1,2,0:T(1,128)S(1)}, u32[]{:S(2)}, u32[]{:S(2)}) collective-permute-start(f32[1,1,3,16384]{3,1,2,0:T(1,128)S(1)} %broadcast_in_dim.28), channel_id=1, source_target_pairs={{16,0},{32,16},{48,32},{64,48},{80,64},{96,80},{112,96},{17,1},{33... | collective-permute-start | bytes 589832 | tf_op jit(solution)/shard_map/ppermute | solution.py:18
  14.2 16.3 %collective-permute-start.17 = (bf16[1,1,32,16384]{3,2,1,0:T(8,128)(2,1)}, bf16[1,1,32,16384]{3,2,1,0:T(8,128)(2,1)S(1)}, u32[]{:S(2)}, u32[]{:S(2)}) collective-permute-start(bf16[1,1,32,16384]{3,2,1,0:T(8,128)(2,1)} %bitcast.201), channel_id=1, source_target_pairs={{16,0},{32,16},{48,32},{64,48},{80,64},{96,80},{112,96},{17,1},{33... | collective-permute-start | bytes 3145736 | tf_op jit(solution)/shard_map/ppermute | solution.py:18
  16.1 15.7 %collective-permute-start.16 = (bf16[1,1,32,16384]{3,2,1,0:T(8,128)(2,1)}, bf16[1,1,32,16384]{3,2,1,0:T(8,128)(2,1)S(1)}, u32[]{:S(2)}, u32[]{:S(2)}) collective-permute-start(bf16[1,1,32,16384]{3,2,1,0:T(8,128)(2,1)} %bitcast.202), channel_id=1, source_target_pairs={{0,16},{16,32},{32,48},{48,64},{64,80},{80,96},{96,112},{1,17},{17... | collective-permute-start | bytes 3145736 | tf_op jit(solution)/shard_map/ppermute | solution.py:17
  19.8 33.6 %collective-permute-start.1 = (bf16[1,1,64,16384]{3,2,1,0:T(8,128)(2,1)}, bf16[1,1,64,16384]{3,2,1,0:T(8,128)(2,1)S(1)}, u32[]{:S(2)}, u32[]{:S(2)}) collective-permute-start(bf16[1,1,64,16384]{3,2,1,0:T(8,128)(2,1)} %bitcast.206), channel_id=1, source_target_pairs={{16,0},{32,16},{48,32},{64,48},{80,64},{96,80},{112,96},{17,1},{33... | collective-permute-start | bytes 6291464 | tf_op jit(solution)/shard_map/ppermute | solution.py:18
  21.7 32.6 %collective-permute-start = (bf16[1,1,64,16384]{3,2,1,0:T(8,128)(2,1)}, bf16[1,1,64,16384]{3,2,1,0:T(8,128)(2,1)S(1)}, u32[]{:S(2)}, u32[]{:S(2)}) collective-permute-start(bf16[1,1,64,16384]{3,2,1,0:T(8,128)(2,1)} %bitcast.207), channel_id=1, source_target_pairs={{0,16},{16,32},{32,48},{48,64},{64,80},{80,96},{96,112},{1,17},{17... | collective-permute-start | bytes 6291464 | tf_op jit(solution)/shard_map/ppermute | solution.py:17
  35.4 32.3 %copy-start.18 = (s32[2,384]{1,0:T(2,128)S(1)}, s32[2,384]{1,0:T(2,128)}, u32[]{:S(2)}) copy-start(s32[2,384]{1,0:T(2,128)} %param.17) | copy-start | bytes 9220
  35.4 32.4 %copy-start.15 = (f32[3,32]{1,0:T(4,128)S(1)}, f32[3,32]{1,0:T(4,128)}, u32[]{:S(2)}) copy-start(f32[3,32]{1,0:T(4,128)} %param.16) | copy-start | bytes 1156
  35.4 34.0 %copy-start.9 = (f32[32,2048]{1,0:T(8,128)S(1)}, f32[32,2048]{1,0:T(8,128)}, u32[]{:S(2)}) copy-start(f32[32,2048]{1,0:T(8,128)} %param.14) | copy-start | bytes 786436
  35.4 218.3 %copy-start.17 = (s32[64,8]{0,1:T(8,128)S(1)}, s32[64,8]{0,1:T(8,128)}, u32[]{:S(2)}) copy-start(s32[64,8]{0,1:T(8,128)} %param.18) | copy-start | bytes 6148
  35.5 235.8 %collective-permute-start.19 = (bf16[3,1,32,16384]{3,2,1,0:T(8,128)(2,1)}, bf16[3,1,32,16384]{3,2,1,0:T(8,128)(2,1)}, u32[]{:S(2)}, u32[]{:S(2)}) collective-permute-start(bf16[3,1,32,16384]{3,2,1,0:T(8,128)(2,1)} %pad_maximum_fusion.3), channel_id=1, source_target_pairs={{1,0},{2,1},{3,2},{4,3},{5,4},{6,5},{7,6},{8,7},{9,8},{10,9},{11,1... | collective-permute-start | bytes 9437192 | tf_op jit(solution)/shard_map/ppermute | solution.py:18
  36.9 244.9 %collective-permute-start.18 = (bf16[3,1,32,16384]{3,2,1,0:T(8,128)(2,1)}, bf16[3,1,32,16384]{3,2,1,0:T(8,128)(2,1)}, u32[]{:S(2)}, u32[]{:S(2)}) collective-permute-start(bf16[3,1,32,16384]{3,2,1,0:T(8,128)(2,1)} %pad_maximum_fusion.3), channel_id=1, source_target_pairs={{0,1},{1,2},{2,3},{3,4},{4,5},{5,6},{6,7},{7,8},{8,9},{9,10},{10,1... | collective-permute-start | bytes 9437192 | tf_op jit(solution)/shard_map/ppermute | solution.py:17
  57.8 242.4 %collective-permute-start.3 = (bf16[3,1,64,16384]{3,2,1,0:T(8,128)(2,1)}, bf16[3,1,64,16384]{3,2,1,0:T(8,128)(2,1)}, u32[]{:S(2)}, u32[]{:S(2)}) collective-permute-start(bf16[3,1,64,16384]{3,2,1,0:T(8,128)(2,1)} %pad_maximum_fusion.2), channel_id=1, source_target_pairs={{1,0},{2,1},{3,2},{4,3},{5,4},{6,5},{7,6},{8,7},{9,8},{10,9},{11,1... | collective-permute-start | bytes 18874376 | tf_op jit(solution)/shard_map/ppermute | solution.py:18
  59.1 241.1 %collective-permute-start.2 = (bf16[3,1,64,16384]{3,2,1,0:T(8,128)(2,1)}, bf16[3,1,64,16384]{3,2,1,0:T(8,128)(2,1)}, u32[]{:S(2)}, u32[]{:S(2)}) collective-permute-start(bf16[3,1,64,16384]{3,2,1,0:T(8,128)(2,1)} %pad_maximum_fusion.2), channel_id=1, source_target_pairs={{0,1},{1,2},{2,3},{3,4},{4,5},{5,6},{6,7},{7,8},{8,9},{9,10},{10,1... | collective-permute-start | bytes 18874376 | tf_op jit(solution)/shard_map/ppermute | solution.py:17
  66.4 184.1 %collective-permute-start.7 = (f32[3,1,3,16384]{3,1,2,0:T(1,128)}, f32[3,1,3,16384]{3,1,2,0:T(1,128)}, u32[]{:S(2)}, u32[]{:S(2)}) collective-permute-start(f32[3,1,3,16384]{3,1,2,0:T(1,128)} %constant_dynamic-update-slice_fusion), channel_id=1, source_target_pairs={{1,0},{2,1},{3,2},{4,3},{5,4},{6,5},{7,6},{8,7},{9,8},{10,9},{11,1... | collective-permute-start | bytes 1769480 | tf_op jit(solution)/shard_map/ppermute | solution.py:18
  250.5 13.2 %collective-permute-start.6 = (f32[3,1,3,16384]{3,1,2,0:T(1,128)}, f32[3,1,3,16384]{3,1,2,0:T(1,128)S(1)}, u32[]{:S(2)}, u32[]{:S(2)}) collective-permute-start(f32[3,1,3,16384]{3,1,2,0:T(1,128)} %constant_dynamic-update-slice_fusion), channel_id=1, source_target_pairs={{0,1},{1,2},{2,3},{3,4},{4,5},{5,6},{6,7},{7,8},{8,9},{9,10},{10,1... | collective-permute-start | bytes 1769480 | tf_op jit(solution)/shard_map/ppermute | solution.py:17
  263.7 513.5 %collective-permute-start.21 = (f32[1,1,3,2048]{3,2,1,0:T(4,128)}, f32[1,1,3,2048]{3,2,1,0:T(4,128)}, u32[]{:S(2)}, u32[]{:S(2)}) collective-permute-start(f32[1,1,3,2048]{3,2,1,0:T(4,128)} %bitcast.21), channel_id=1, source_target_pairs={{16,0},{32,16},{48,32},{64,48},{80,64},{96,80},{112,96},{17,1},{33... | collective-permute-start | bytes 73736 | tf_op jit(solution)/shard_map/ppermute | solution.py:18
  271.3 505.8 %collective-permute-start.20 = (f32[1,1,3,2048]{3,2,1,0:T(4,128)}, f32[1,1,3,2048]{3,2,1,0:T(4,128)}, u32[]{:S(2)}, u32[]{:S(2)}) collective-permute-start(f32[1,1,3,2048]{3,2,1,0:T(4,128)} %bitcast.21), channel_id=1, source_target_pairs={{0,16},{16,32},{32,48},{48,64},{64,80},{80,96},{96,112},{1,17},{17... | collective-permute-start | bytes 73736 | tf_op jit(solution)/shard_map/ppermute | solution.py:17
  734.9 66.7 %collective-permute-start.8 = (bf16[64,16384]{1,0:T(8,128)(2,1)}, bf16[64,16384]{1,0:T(8,128)(2,1)}, u32[]{:S(2)}, u32[]{:S(2)}) collective-permute-start(bf16[64,16384]{1,0:T(8,128)(2,1)} %get-tuple-element.115), channel_id=1, source_target_pairs={{17,0},{18,1},{19,2},{20,3},{21,4},{22,5},{23,6},{24,7},{25,8},{26... | collective-permute-start | bytes 6291464 | tf_op jit(solution)/shard_map/ppermute | solution.py:26
  736.2 72.4 %collective-permute-start.15 = (bf16[64,16384]{1,0:T(8,128)(2,1)}, bf16[64,16384]{1,0:T(8,128)(2,1)}, u32[]{:S(2)}, u32[]{:S(2)}) collective-permute-start(bf16[64,16384]{1,0:T(8,128)(2,1)} %get-tuple-element.116), channel_id=1, source_target_pairs={{0,17},{1,18},{2,19},{3,20},{4,21},{5,22},{6,23},{7,24},{8,25},{9,... | collective-permute-start | bytes 6291464 | tf_op jit(solution)/shard_map/ppermute | solution.py:26
  742.8 68.8 %collective-permute-start.14 = (bf16[64,16384]{1,0:T(8,128)(2,1)}, bf16[64,16384]{1,0:T(8,128)(2,1)}, u32[]{:S(2)}, u32[]{:S(2)}) collective-permute-start(bf16[64,16384]{1,0:T(8,128)(2,1)} %get-tuple-element.117), channel_id=1, source_target_pairs={{0,16},{1,17},{2,18},{3,19},{4,20},{5,21},{6,22},{7,23},{8,24},{9,... | collective-permute-start | bytes 6291464 | tf_op jit(solution)/shard_map/ppermute | solution.py:26
  744.9 32.0 %copy-start.19 = (s32[1,16]{1,0:T(1,128)S(1)}, s32[1,16]{1,0:T(1,128)}, u32[]{:S(2)}) copy-start(s32[1,16]{1,0:T(1,128)} %param.19) | copy-start | bytes 196
  744.9 32.0 %copy-start.14 = (s32[64,8]{0,1:T(8,128)S(1)}, s32[64,8]{0,1:T(8,128)}, u32[]{:S(2)}) copy-start(s32[64,8]{0,1:T(8,128)} %fusion.107) | copy-start | bytes 6148
  778.0 9.3 collective-permute-start.23
  779.3 8.0 collective-permute-start.22
  791.6 144.5 %collective-permute-start.13 = (bf16[64,16384]{1,0:T(8,128)(2,1)}, bf16[64,16384]{1,0:T(8,128)(2,1)}, u32[]{:S(2)}, u32[]{:S(2)}) collective-permute-start(bf16[64,16384]{1,0:T(8,128)(2,1)} %get-tuple-element.118), channel_id=1, source_target_pairs={{0,15},{1,16},{2,17},{3,18},{4,19},{5,20},{6,21},{7,22},{8,23},{9,... | collective-permute-start | bytes 6291464 | tf_op jit(solution)/shard_map/ppermute | solution.py:26
  799.7 136.4 %collective-permute-start.12 = (bf16[64,16384]{1,0:T(8,128)(2,1)}, bf16[64,16384]{1,0:T(8,128)(2,1)}, u32[]{:S(2)}, u32[]{:S(2)}) collective-permute-start(bf16[64,16384]{1,0:T(8,128)(2,1)} %get-tuple-element.119), channel_id=1, source_target_pairs={{0,1},{1,2},{2,3},{3,4},{4,5},{5,6},{6,7},{7,8},{8,9},{9,10},{10,1... | collective-permute-start | bytes 6291464 | tf_op jit(solution)/shard_map/ppermute | solution.py:26
  801.6 134.5 %collective-permute-start.11 = (bf16[64,16384]{1,0:T(8,128)(2,1)}, bf16[64,16384]{1,0:T(8,128)(2,1)}, u32[]{:S(2)}, u32[]{:S(2)}) collective-permute-start(bf16[64,16384]{1,0:T(8,128)(2,1)} %get-tuple-element.120), channel_id=1, source_target_pairs={{1,0},{2,1},{3,2},{4,3},{5,4},{6,5},{7,6},{8,7},{9,8},{10,9},{11,1... | collective-permute-start | bytes 6291464 | tf_op jit(solution)/shard_map/ppermute | solution.py:26
  808.6 127.5 %collective-permute-start.10 = (bf16[64,16384]{1,0:T(8,128)(2,1)}, bf16[64,16384]{1,0:T(8,128)(2,1)}, u32[]{:S(2)}, u32[]{:S(2)}) collective-permute-start(bf16[64,16384]{1,0:T(8,128)(2,1)} %get-tuple-element.121), channel_id=1, source_target_pairs={{15,0},{16,1},{17,2},{18,3},{19,4},{20,5},{21,6},{22,7},{23,8},{24... | collective-permute-start | bytes 6291464 | tf_op jit(solution)/shard_map/ppermute | solution.py:26
  811.6 124.5 %collective-permute-start.9 = (bf16[64,16384]{1,0:T(8,128)(2,1)}, bf16[64,16384]{1,0:T(8,128)(2,1)}, u32[]{:S(2)}, u32[]{:S(2)}) collective-permute-start(bf16[64,16384]{1,0:T(8,128)(2,1)} %get-tuple-element.122), channel_id=1, source_target_pairs={{16,0},{17,1},{18,2},{19,3},{20,4},{21,5},{22,6},{23,7},{24,8},{25... | collective-permute-start | bytes 6291464 | tf_op jit(solution)/shard_map/ppermute | solution.py:26
  (13 other events, 208.6 us)
Sparse Core Ops, SparseCore 0:
  777.0 145.1 all-gather.1
where the time goes:
time: 964 us; the launch traced here: 953 us
  local copies, waits for them, and re-layouts  298 us (31%)
  waiting for transfers between devices  295 us (31%)
  matrix products  130 us (13%)
  other arithmetic  128 us (13%)
  starting transfers between devices  86.8 us (9%)
  between operations  14.2 us (1%)
    ppermute x8, waiting for transfers between devices, with_halo(): after = lax.ppermute(initial, axis, down)  197 us
    all_gather x1, waiting for transfers between devices, turned_gather(): result, at, outs = (lax.all_gather(both, axis, axis=0, tiled=True), 0, [])  87.4 us
    gather x12, local copies, waits for them, and re-layouts, near_step(): src_vectors = vectors_pool[s_hood, :, s_leaf, :]  83.9 us
    dot_general x12, matrix products, near_step(): jnp.einsum('bvs,bts->bvt', src_vectors, block, preferred_element_type=jnp...  83.5 us
    scatter-add x12, other arithmetic, near_step(): return (buffer.at[t_hood, :, t_leaf, :].add(partial_value), None)  77 us
    while x2, local copies, waits for them, and re-layouts, shards(): lax.scan(near_step, start, (tgt_hood, tgt_leaf, src_hood, src_leaf))  47.3 us
    ppermute x8, starting transfers between devices, with_halo(): before = lax.ppermute(last, axis, up)  41.9 us
    reshape x1, local copies, waits for them, and re-layouts, shards(): buffer = buffer.reshape(3, 3, vec_count, leaves * leaf_width)  40.3 us
  transfers between devices with their start and end apart: 25, of which 8 were waited for; matrix products, arithmetic and copies ran while one was open for 57% of the time, Pallas kernels for 0%

commit v1 on v0

--- a/solution.py
+++ b/solution.py
@@ -5,6 +5,11 @@
 from jax.sharding import PartitionSpec as P
 
 HIGH = lax.Precision.HIGHEST
+
+
+def gather_over(array, axis, dim):
+    stack = jnp.stack([array] * lax.axis_size(axis))
+    return jnp.concatenate(lax.all_to_all(stack, axis, 0, 0), axis=dim)
 
 
 def with_halo(array, sides, width):
@@ -29,7 +34,7 @@
 def turned_gather(arrays, axis, dims):
     turned = [jnp.moveaxis(a, dim, 0) for a, dim in zip(arrays, dims)]
     both = jnp.concatenate([t.reshape(len(t), -1) for t in turned], axis=1)
-    result, at, outs = (lax.all_gather(both, axis, axis=0, tiled=True), 0, [])
+    result, at, outs = (gather_over(both, axis, 0), 0, [])
     for t, dim in zip(turned, dims):
         share = result[:, at : at + t[0].size].reshape(-1, *t.shape[1:])
         outs.append(jnp.moveaxis(share, 0, dim))

time: 964 us -> 919 us (0.953)
  waiting for transfers between devices: 295 us -> 198 us
  starting transfers between devices: 86.8 us -> 116 us
  other arithmetic: 128 us -> 145 us
  between operations: 14.2 us -> 0.81 us
  local copies, waits for them, and re-layouts: 298 us -> 310 us
    all_gather x1 -> x0, waiting for transfers between devices: 87.4 us -> none  [turned_gather(): result, at, outs = (lax.all_gather(both, axis, axis=0, tiled=True), 0, [])]
    ppermute x8, waiting for transfers between devices: 197 us -> 129 us  [with_halo(): after = lax.ppermute(initial, axis, down)]
    ppermute x8, waiting for transfers between devices: 0.02 us -> 55.6 us  [from_behind(): return lax.ppermute(block, axis, route)]
    all_to_all x0 -> x1, starting transfers between devices: none -> 14.9 us  [gather_over(): return jnp.concatenate(lax.all_to_all(stack, axis, 0, 0), axis=dim)]
    ppermute x8, starting transfers between devices: 41.9 us -> 56.4 us  [with_halo(): before = lax.ppermute(last, axis, up)]
  transfers between devices with their start and end apart: 25 -> 25, of which waited for: 8 -> 7; matrix products, arithmetic and copies ran while one was open for 57% -> 64% of each run, Pallas kernels for 0% -> 0%
where the time goes in v1:
time: 919 us; the launch traced here: 903 us
  local copies, waits for them, and re-layouts  310 us (34%)
  waiting for transfers between devices  198 us (22%)
  other arithmetic  145 us (16%)
  matrix products  132 us (14%)
  starting transfers between devices  116 us (13%)
    ppermute x8, waiting for transfers between devices, with_halo(): after = lax.ppermute(initial, axis, down)  129 us
    gather x12, local copies, waits for them, and re-layouts, near_step(): src_vectors = vectors_pool[s_hood, :, s_leaf, :]  83.9 us
    dot_general x12, matrix products, near_step(): jnp.einsum('bvs,bts->bvt', src_vectors, block, preferred_element_type=jnp...  83.5 us
    scatter-add x12, other arithmetic, near_step(): return (buffer.at[t_hood, :, t_leaf, :].add(partial_value), None)  77.3 us
    ppermute x8, starting transfers between devices, with_halo(): before = lax.ppermute(last, axis, up)  56.4 us
    ppermute x8, waiting for transfers between devices, from_behind(): return lax.ppermute(block, axis, route)  55.6 us
    while x2, local copies, waits for them, and re-layouts, shards(): lax.scan(near_step, start, (tgt_hood, tgt_leaf, src_hood, src_leaf))  47.3 us
    reshape x1, local copies, waits for them, and re-layouts, shards(): buffer = buffer.reshape(3, 3, vec_count, leaves * leaf_width)  40.3 us
  transfers between devices with their start and end apart: 25, of which 7 were waited for; matrix products, arithmetic and copies ran while one was open for 64% of the time, Pallas kernels for 0%

profile of v1, /device:TPU:1, one launch (start us, length us, event | category | flops | bytes accessed | tf_op | source)
XLA Modules:
  0.0 902.9 jit_solution(13842670834198463821)
XLA Ops:
  27.0 14.7 %collective-permute-done.1 = bf16[1,1,64,16384]{3,2,1,0:T(8,128)(2,1)S(1)} collective-permute-done((bf16[1,1,64,16384]{3,2,1,0:T(8,128)(2,1)}, bf16[1,1,64,16384]{3,2,1,0:T(8,128)(2,1)S(1)}, u32[]{:S(2)}, u32[]{:S(2)}) %collective-permute-start.1) | collective-permute-done | bytes 2097184 | tf_op jit(solution)/shard_map/ppermute | solution.py:23
  72.9 114.2 %collective-permute-done.23 = f32[3,1,3,2048]{3,2,1,0:T(4,128)} collective-permute-done((f32[3,1,3,2048]{3,2,1,0:T(4,128)}, f32[3,1,3,2048]{3,2,1,0:T(4,128)}, u32[]{:S(2)}, u32[]{:S(2)}) %collective-permute-start.23) | collective-permute-done | bytes 73760 | tf_op jit(solution)/shard_map/ppermute | solution.py:23
  205.5 24.6 %collective-permute-start.16 = (bf16[1,1,32,16384]{3,2,1,0:T(8,128)(2,1)S(1)}, bf16[1,1,32,16384]{3,2,1,0:T(8,128)(2,1)S(1)}, u32[]{:S(2)}, u32[]{:S(2)}) collective-permute-start(bf16[1,1,32,16384]{3,2,1,0:T(8,128)(2,1)S(1)} %bitcast.205), channel_id=1, source_target_pairs={{0,16},{16,32},{32,48},{48,64},{64,80},{80,96},{96,112},{1,17},{17... | collective-permute-start | bytes 3145736 | tf_op jit(solution)/shard_map/ppermute | solution.py:22
  253.4 11.9 %pad_maximum_fusion = bf16[3,3,64,16384]{3,2,1,0:T(8,128)(2,1)S(1)} fusion(bf16[3,1,64,16384]{3,2,1,0:T(8,128)(2,1)} %collective-permute-done.3, bf16[1,1,64,16384]{3,2,1,0:T(8,128)(2,1)S(1)} %collective-permute-done.1, bf16[1,1,64,16384]{3,2,1,0:T(8,128)(2,1)S(1)} %bitcast.212, bf16[1,1,64,16384]{3,2,1,0:T(8,128)(2,1)S(1)} %copy-done.9, ...), kind=kLoop, calls=%fused_computation.43 | loop fusion | flops 37748736 | bytes 37748736 | tf_op jit(solution)/shard_map/concatenate | solution.py:24
  269.8 12.0 %copy.79 = bf16[9,64,64,256]{3,1,2,0:T(8,128)(2,1)} copy(bf16[9,64,64,256]{3,2,1,0:T(8,128)(2,1)S(1)} %bitcast.195) | data formatting | bytes 37748736 | tf_op jit(solution)/shard_map/while | solution.py:115
  281.9 12.6 %broadcast_in_dim.26 = f32[9,64,64,256]{3,1,2,0:T(8,128)} broadcast(f32[]{:T(128)} %constant.129.clone.1), dimensions={} | broadcast | bytes 37748740 | tf_op jit(solution)/shard_map/broadcast_in_dim | solution.py:114
  294.5 312.4 %while.10 = (s32[]{:T(128)}, f32[9,64,64,256]{3,1,2,0:T(8,128)}, s32[12,32]{1,0:T(8,128)}, s32[12,32]{1,0:T(8,128)}, s32[12,32]{1,0:T(8,128)}, /*index=5*/s32[12...) while((s32[]{:T(128)}, f32[9,64,64,256]{3,1,2,0:T(8,128)}, ...), condition=%wide.region_2.3_spmd, body=%wide.region_0.2_spmd.sunk | while | flops 289932096 | bytes 12912617 | solution.py:115
  300.1 7.0 gather_fusion
  326.2 7.0 gather_fusion
  352.2 7.0 gather_fusion
  378.2 7.0 gather_fusion
  404.2 7.0 gather_fusion
  430.3 7.0 gather_fusion
  456.3 7.0 gather_fusion
  482.3 7.0 gather_fusion
  508.3 7.0 gather_fusion
  534.4 7.0 gather_fusion
  560.4 7.0 gather_fusion
  606.9 35.3 %copy.81 = f32[9,64,64,256]{3,2,1,0:T(8,128)} copy(f32[9,64,64,256]{3,1,2,0:T(8,128)} %get-tuple-element.47) | data formatting | bytes 75497472 | tf_op jit(solution)/shard_map/while | solution.py:115
  642.2 40.3 %reshape.198 = f32[3,3,64,16384]{3,2,1,0:T(8,128)} reshape(f32[9,64,64,256]{3,2,1,0:T(8,128)} %copy.81) | data formatting | bytes 75497472 | tf_op jit(solution)/shard_map/reshape | solution.py:116
  682.5 13.1 %convert.10 = bf16[3,3,64,16384]{3,2,1,0:T(8,128)(2,1)S(1)} convert(f32[3,3,64,16384]{3,2,1,0:T(8,128)} %reshape.198) | non-fusion elementwise | flops 9437184 | bytes 56623104 | tf_op jit(solution)/shard_map/convert.7
  702.8 7.4 collective-permute-start.15
  712.1 8.3 pad_maximum_fusion.1
  720.4 10.5 %copy.105 = bf16[36,8,64,256]{3,2,1,0:T(8,128)(2,1)} copy(bf16[36,8,64,256]{3,1,2,0:T(8,128)(2,1)} %bitcast.198) | data formatting | bytes 18874368
  731.0 29.1 %convert_bitcast_fusion = bf16[9,64,64,32]{1,3,2,0:T(8,128)(2,1)} fusion(bf16[9,32,64,256]{3,2,1,0:T(8,128)(2,1)} %bitcast.203, bf16[9,64,64,256]{3,2,1,0:T(8,128)(2,1)} %bitcast.196), kind=kOutput, calls=%fused_computation.59 | convolution fusion | flops 605159424 | bytes 30670848 | tf_op jit(solution)/shard_map/nvil,nril->nvir/dot_general | solution.py:54
  764.1 14.9 %all-to-all-start = ((f32[128,32,67]{2,1,0:T(8,128)}), f32[128,32,67]{2,1,0:T(8,128)S(1)}, u32[]{:S(2)}, u32[]{:S(2)}) async-start(f32[128,32,67]{2,1,0:T(8,128)} %stack.2), calls=%async_computation | async-start | bytes 4194304 | tf_op jit(solution)/shard_map/all_to_all | solution.py:12
  779.0 7.5 collective-permute-start.13
  802.9 8.4 gather_fusion.3
  811.3 13.3 %fusion.47 = f32[64,64,32]{1,2,0:T(8,128)} fusion(bf16[64,8,64,32]{2,3,1,0:T(8,128)(2,1)} %bitcast.200, f32[64,32]{1,0:T(8,128)S(1)} %copy-done.16, f32[64,8,32]{2,1,0:T(8,128)} %bitcast.228, f32[64,32]{1,0:T(8,128)S(1)} %copy-done.17, f32[64,8,32]{2,1,0:T(8,128)} %bitcast.227, f32[64,32]{1,0:T(8,128)S(1)} %copy-done.15, f32[64,8,32]{2,1,0:T(8,128)S(1)} %bitcast.226), kind=kOutput, calls=%fused_computation.88 | convolution fusion | flops 407371776 | bytes 2842624 | tf_op jit(solution)/shard_map/ifvs,ifst->ivt/dot_general | solution.py:131
  836.8 32.9 %collective-permute-done.13 = bf16[64,16384]{1,0:T(8,128)(2,1)} collective-permute-done((bf16[64,16384]{1,0:T(8,128)(2,1)}, bf16[64,16384]{1,0:T(8,128)(2,1)}, u32[]{:S(2)}, u32[]{:S(2)}) %collective-permute-start.13) | collective-permute-done | bytes 2097184 | tf_op jit(solution)/shard_map/ppermute | solution.py:31
  869.7 22.7 %collective-permute-done.11 = bf16[64,16384]{1,0:T(8,128)(2,1)} collective-permute-done((bf16[64,16384]{1,0:T(8,128)(2,1)}, bf16[64,16384]{1,0:T(8,128)(2,1)}, u32[]{:S(2)}, u32[]{:S(2)}) %collective-permute-start.11) | collective-permute-done | bytes 2097184 | tf_op jit(solution)/shard_map/ppermute | solution.py:31
  892.4 10.2 %fusion.37 = f32[64,16384]{1,0:T(8,128)} fusion(f32[64,16384]{1,0:T(8,128)S(1)} %bitcast.199, f32[3,3,64,16384]{3,2,1,0:T(8,128)} %reshape.198, bf16[64,16384]{1,0:T(8,128)(2,1)} %collective-permute-done.15, bf16[64,16384]{1,0:T(8,128)(2,1)} %collective-permute-done.14, bf16[64,16384]{1,0:T(8,128)(2,1)} %collective-permute-done.13, ...), kind=kLoop, calls=%fused_computation.69 | loop fusion | flops 17825792 | bytes 29360128 | tf_op jit(solution)/shard_map/add | solution.py:152
  (287 shorter events, 380.3 us)
Async XLA Ops:
  0.0 63.8 %collective-permute-start.21 = (f32[1,1,3,2048]{3,2,1,0:T(4,128)}, f32[1,1,3,2048]{3,2,1,0:T(4,128)S(1)}, u32[]{:S(2)}, u32[]{:S(2)}) collective-permute-start(f32[1,1,3,2048]{3,2,1,0:T(4,128)} %bitcast.222), channel_id=1, source_target_pairs={{16,0},{32,16},{48,32},{64,48},{80,64},{96,80},{112,96},{17,1},{33... | collective-permute-start | bytes 73736 | tf_op jit(solution)/shard_map/ppermute | solution.py:23
  3.3 65.4 %collective-permute-start.20 = (f32[1,1,3,2048]{3,2,1,0:T(4,128)}, f32[1,1,3,2048]{3,2,1,0:T(4,128)S(1)}, u32[]{:S(2)}, u32[]{:S(2)}) collective-permute-start(f32[1,1,3,2048]{3,2,1,0:T(4,128)} %bitcast.223), channel_id=1, source_target_pairs={{0,16},{16,32},{32,48},{48,64},{64,80},{80,96},{96,112},{1,17},{17... | collective-permute-start | bytes 73736 | tf_op jit(solution)/shard_map/ppermute | solution.py:22
  8.2 52.7 %collective-permute-start.5 = (f32[1,1,3,16384]{3,1,2,0:T(1,128)}, f32[1,1,3,16384]{3,1,2,0:T(1,128)}, u32[]{:S(2)}, u32[]{:S(2)}) collective-permute-start(f32[1,1,3,16384]{3,1,2,0:T(1,128)} %broadcast_in_dim.28), channel_id=1, source_target_pairs={{16,0},{32,16},{48,32},{64,48},{80,64},{96,80},{112,96},{17,1},{33... | collective-permute-start | bytes 589832 | tf_op jit(solution)/shard_map/ppermute | solution.py:23
  10.1 10.8 %collective-permute-start.4 = (f32[1,1,3,16384]{3,1,2,0:T(1,128)}, f32[1,1,3,16384]{3,1,2,0:T(1,128)S(1)}, u32[]{:S(2)}, u32[]{:S(2)}) collective-permute-start(f32[1,1,3,16384]{3,1,2,0:T(1,128)} %broadcast_in_dim.28), channel_id=1, source_target_pairs={{0,16},{16,32},{32,48},{48,64},{64,80},{80,96},{96,112},{1,17},{17... | collective-permute-start | bytes 589832 | tf_op jit(solution)/shard_map/ppermute | solution.py:22
  13.8 28.0 %collective-permute-start.1 = (bf16[1,1,64,16384]{3,2,1,0:T(8,128)(2,1)}, bf16[1,1,64,16384]{3,2,1,0:T(8,128)(2,1)S(1)}, u32[]{:S(2)}, u32[]{:S(2)}) collective-permute-start(bf16[1,1,64,16384]{3,2,1,0:T(8,128)(2,1)} %bitcast.209), channel_id=1, source_target_pairs={{16,0},{32,16},{48,32},{64,48},{80,64},{96,80},{112,96},{17,1},{33... | collective-permute-start | bytes 6291464 | tf_op jit(solution)/shard_map/ppermute | solution.py:23
  20.9 26.9 %collective-permute-start = (bf16[1,1,64,16384]{3,2,1,0:T(8,128)(2,1)}, bf16[1,1,64,16384]{3,2,1,0:T(8,128)(2,1)S(1)}, u32[]{:S(2)}, u32[]{:S(2)}) collective-permute-start(bf16[1,1,64,16384]{3,2,1,0:T(8,128)(2,1)} %bitcast.210), channel_id=1, source_target_pairs={{0,16},{16,32},{32,48},{48,64},{64,80},{80,96},{96,112},{1,17},{17... | collective-permute-start | bytes 6291464 | tf_op jit(solution)/shard_map/ppermute | solution.py:22
  27.0 41.7 %copy-start.12 = (f32[3,2048]{1,0:T(4,128)S(1)}, f32[3,2048]{1,0:T(4,128)}, u32[]{:S(2)}) copy-start(f32[3,2048]{1,0:T(4,128)} %param.15) | copy-start | bytes 73732
  27.0 43.7 %copy-start.22 = (s32[1,16]{1,0:T(1,128)S(1)}, s32[1,16]{1,0:T(1,128)}, u32[]{:S(2)}) copy-start(s32[1,16]{1,0:T(1,128)} %param.19) | copy-start | bytes 196
  27.0 43.7 %copy-start.18 = (f32[3,32]{1,0:T(4,128)S(1)}, f32[3,32]{1,0:T(4,128)}, u32[]{:S(2)}) copy-start(f32[3,32]{1,0:T(4,128)} %param.16) | copy-start | bytes 1156
  27.0 44.6 %copy-start.13 = (f32[32,2048]{1,0:T(8,128)S(1)}, f32[32,2048]{1,0:T(8,128)}, u32[]{:S(2)}) copy-start(f32[32,2048]{1,0:T(8,128)} %param.14) | copy-start | bytes 786436
  27.0 165.3 %copy-start.4 = (bf16[32,16384]{1,0:T(8,128)(2,1)S(1)}, bf16[32,16384]{1,0:T(8,128)(2,1)}, u32[]{:S(2)}) copy-start(bf16[32,16384]{1,0:T(8,128)(2,1)} %param.13) | copy-start | bytes 3145732
  53.0 200.4 %collective-permute-start.3 = (bf16[3,1,64,16384]{3,2,1,0:T(8,128)(2,1)}, bf16[3,1,64,16384]{3,2,1,0:T(8,128)(2,1)}, u32[]{:S(2)}, u32[]{:S(2)}) collective-permute-start(bf16[3,1,64,16384]{3,2,1,0:T(8,128)(2,1)} %pad_maximum_fusion.2), channel_id=1, source_target_pairs={{1,0},{2,1},{3,2},{4,3},{5,4},{6,5},{7,6},{8,7},{9,8},{10,9},{11,1... | collective-permute-start | bytes 18874376 | tf_op jit(solution)/shard_map/ppermute | solution.py:23
  54.3 199.1 %collective-permute-start.2 = (bf16[3,1,64,16384]{3,2,1,0:T(8,128)(2,1)}, bf16[3,1,64,16384]{3,2,1,0:T(8,128)(2,1)}, u32[]{:S(2)}, u32[]{:S(2)}) collective-permute-start(bf16[3,1,64,16384]{3,2,1,0:T(8,128)(2,1)} %pad_maximum_fusion.2), channel_id=1, source_target_pairs={{0,1},{1,2},{2,3},{3,4},{4,5},{5,6},{6,7},{7,8},{8,9},{9,10},{10,1... | collective-permute-start | bytes 18874376 | tf_op jit(solution)/shard_map/ppermute | solution.py:22
  62.6 142.9 %collective-permute-start.7 = (f32[3,1,3,16384]{3,1,2,0:T(1,128)}, f32[3,1,3,16384]{3,1,2,0:T(1,128)}, u32[]{:S(2)}, u32[]{:S(2)}) collective-permute-start(f32[3,1,3,16384]{3,1,2,0:T(1,128)} %constant_dynamic-update-slice_fusion), channel_id=1, source_target_pairs={{1,0},{2,1},{3,2},{4,3},{5,4},{6,5},{7,6},{8,7},{9,8},{10,9},{11,1... | collective-permute-start | bytes 1769480 | tf_op jit(solution)/shard_map/ppermute | solution.py:23
  63.9 166.2 %collective-permute-start.6 = (f32[3,1,3,16384]{3,1,2,0:T(1,128)}, f32[3,1,3,16384]{3,1,2,0:T(1,128)}, u32[]{:S(2)}, u32[]{:S(2)}) collective-permute-start(f32[3,1,3,16384]{3,1,2,0:T(1,128)} %constant_dynamic-update-slice_fusion), channel_id=1, source_target_pairs={{0,1},{1,2},{2,3},{3,4},{4,5},{5,6},{6,7},{7,8},{8,9},{9,10},{10,1... | collective-permute-start | bytes 1769480 | tf_op jit(solution)/shard_map/ppermute | solution.py:22
  69.3 117.8 %collective-permute-start.23 = (f32[3,1,3,2048]{3,2,1,0:T(4,128)}, f32[3,1,3,2048]{3,2,1,0:T(4,128)}, u32[]{:S(2)}, u32[]{:S(2)}) collective-permute-start(f32[3,1,3,2048]{3,2,1,0:T(4,128)} %pad_maximum_fusion.6), channel_id=1, source_target_pairs={{1,0},{2,1},{3,2},{4,3},{5,4},{6,5},{7,6},{8,7},{9,8},{10,9},{11,1... | collective-permute-start | bytes 221192 | tf_op jit(solution)/shard_map/ppermute | solution.py:23
  71.5 161.7 %copy-start = (s32[512]{0:T(512)}, s32[512]{0:T(512)S(1)}, u32[]{:S(2)}) copy-start(s32[512]{0:T(512)S(1)} %reshape.226) | copy-start | bytes 6148
  187.1 5.1 collective-permute-start.22
  192.2 43.6 %collective-permute-start.17 = (bf16[1,1,32,16384]{3,2,1,0:T(8,128)(2,1)S(1)}, bf16[1,1,32,16384]{3,2,1,0:T(8,128)(2,1)}, u32[]{:S(2)}, u32[]{:S(2)}) collective-permute-start(bf16[1,1,32,16384]{3,2,1,0:T(8,128)(2,1)S(1)} %bitcast.204), channel_id=1, source_target_pairs={{16,0},{32,16},{48,32},{64,48},{80,64},{96,80},{112,96},{17,1},{33... | collective-permute-start | bytes 3145736 | tf_op jit(solution)/shard_map/ppermute | solution.py:23
  205.5 36.3 %collective-permute-start.16 = (bf16[1,1,32,16384]{3,2,1,0:T(8,128)(2,1)S(1)}, bf16[1,1,32,16384]{3,2,1,0:T(8,128)(2,1)S(1)}, u32[]{:S(2)}, u32[]{:S(2)}) collective-permute-start(bf16[1,1,32,16384]{3,2,1,0:T(8,128)(2,1)S(1)} %bitcast.205), channel_id=1, source_target_pairs={{0,16},{16,32},{32,48},{48,64},{64,80},{80,96},{96,112},{1,17},{17... | collective-permute-start | bytes 3145736 | tf_op jit(solution)/shard_map/ppermute | solution.py:22
  245.4 466.7 %collective-permute-start.19 = (bf16[3,1,32,16384]{3,2,1,0:T(8,128)(2,1)}, bf16[3,1,32,16384]{3,2,1,0:T(8,128)(2,1)}, u32[]{:S(2)}, u32[]{:S(2)}) collective-permute-start(bf16[3,1,32,16384]{3,2,1,0:T(8,128)(2,1)} %pad_maximum_fusion.3), channel_id=1, source_target_pairs={{1,0},{2,1},{3,2},{4,3},{5,4},{6,5},{7,6},{8,7},{9,8},{10,9},{11,1... | collective-permute-start | bytes 9437192 | tf_op jit(solution)/shard_map/ppermute | solution.py:23
  246.7 465.4 %collective-permute-start.18 = (bf16[3,1,32,16384]{3,2,1,0:T(8,128)(2,1)}, bf16[3,1,32,16384]{3,2,1,0:T(8,128)(2,1)}, u32[]{:S(2)}, u32[]{:S(2)}) collective-permute-start(bf16[3,1,32,16384]{3,2,1,0:T(8,128)(2,1)} %pad_maximum_fusion.3), channel_id=1, source_target_pairs={{0,1},{1,2},{2,3},{3,4},{4,5},{5,6},{6,7},{7,8},{8,9},{9,10},{10,1... | collective-permute-start | bytes 9437192 | tf_op jit(solution)/shard_map/ppermute | solution.py:22
  701.5 86.9 %collective-permute-start.8 = (bf16[64,16384]{1,0:T(8,128)(2,1)}, bf16[64,16384]{1,0:T(8,128)(2,1)}, u32[]{:S(2)}, u32[]{:S(2)}) collective-permute-start(bf16[64,16384]{1,0:T(8,128)(2,1)} %get-tuple-element.131), channel_id=1, source_target_pairs={{17,0},{18,1},{19,2},{20,3},{21,4},{22,5},{23,6},{24,7},{25,8},{26... | collective-permute-start | bytes 6291464 | tf_op jit(solution)/shard_map/ppermute | solution.py:31
  702.8 92.6 %collective-permute-start.15 = (bf16[64,16384]{1,0:T(8,128)(2,1)}, bf16[64,16384]{1,0:T(8,128)(2,1)}, u32[]{:S(2)}, u32[]{:S(2)}) collective-permute-start(bf16[64,16384]{1,0:T(8,128)(2,1)} %get-tuple-element.132), channel_id=1, source_target_pairs={{0,17},{1,18},{2,19},{3,20},{4,21},{5,22},{6,23},{7,24},{8,25},{9,... | collective-permute-start | bytes 6291464 | tf_op jit(solution)/shard_map/ppermute | solution.py:31
  710.2 87.2 %collective-permute-start.14 = (bf16[64,16384]{1,0:T(8,128)(2,1)}, bf16[64,16384]{1,0:T(8,128)(2,1)}, u32[]{:S(2)}, u32[]{:S(2)}) collective-permute-start(bf16[64,16384]{1,0:T(8,128)(2,1)} %get-tuple-element.133), channel_id=1, source_target_pairs={{0,16},{1,17},{2,18},{3,19},{4,20},{5,21},{6,22},{7,23},{8,24},{9,... | collective-permute-start | bytes 6291464 | tf_op jit(solution)/shard_map/ppermute | solution.py:31
  762.4 40.5 %copy-start.1 = (s32[512]{0:T(512)S(1)}, s32[512]{0:T(512)}, u32[]{:S(2)}) copy-start(s32[512]{0:T(512)} %copy-done) | copy-start | bytes 6148
  764.1 60.6 %all-to-all-start = ((f32[128,32,67]{2,1,0:T(8,128)}), f32[128,32,67]{2,1,0:T(8,128)S(1)}, u32[]{:S(2)}, u32[]{:S(2)}) async-start(f32[128,32,67]{2,1,0:T(8,128)} %stack.2), calls=%async_computation | async-start | bytes 4194304 | tf_op jit(solution)/shard_map/all_to_all | solution.py:12
  779.0 90.7 %collective-permute-start.13 = (bf16[64,16384]{1,0:T(8,128)(2,1)}, bf16[64,16384]{1,0:T(8,128)(2,1)}, u32[]{:S(2)}, u32[]{:S(2)}) collective-permute-start(bf16[64,16384]{1,0:T(8,128)(2,1)} %get-tuple-element.134), channel_id=1, source_target_pairs={{0,15},{1,16},{2,17},{3,18},{4,19},{5,20},{6,21},{7,22},{8,23},{9,... | collective-permute-start | bytes 6291464 | tf_op jit(solution)/shard_map/ppermute | solution.py:31
  786.5 83.2 %collective-permute-start.12 = (bf16[64,16384]{1,0:T(8,128)(2,1)}, bf16[64,16384]{1,0:T(8,128)(2,1)}, u32[]{:S(2)}, u32[]{:S(2)}) collective-permute-start(bf16[64,16384]{1,0:T(8,128)(2,1)} %get-tuple-element.135), channel_id=1, source_target_pairs={{0,1},{1,2},{2,3},{3,4},{4,5},{5,6},{6,7},{7,8},{8,9},{9,10},{10,1... | collective-permute-start | bytes 6291464 | tf_op jit(solution)/shard_map/ppermute | solution.py:31
  788.4 104.0 %collective-permute-start.11 = (bf16[64,16384]{1,0:T(8,128)(2,1)}, bf16[64,16384]{1,0:T(8,128)(2,1)}, u32[]{:S(2)}, u32[]{:S(2)}) collective-permute-start(bf16[64,16384]{1,0:T(8,128)(2,1)} %get-tuple-element.136), channel_id=1, source_target_pairs={{1,0},{2,1},{3,2},{4,3},{5,4},{6,5},{7,6},{8,7},{9,8},{10,9},{11,1... | collective-permute-start | bytes 6291464 | tf_op jit(solution)/shard_map/ppermute | solution.py:31
  795.4 97.0 %collective-permute-start.10 = (bf16[64,16384]{1,0:T(8,128)(2,1)}, bf16[64,16384]{1,0:T(8,128)(2,1)}, u32[]{:S(2)}, u32[]{:S(2)}) collective-permute-start(bf16[64,16384]{1,0:T(8,128)(2,1)} %get-tuple-element.137), channel_id=1, source_target_pairs={{15,0},{16,1},{17,2},{18,3},{19,4},{20,5},{21,6},{22,7},{23,8},{24... | collective-permute-start | bytes 6291464 | tf_op jit(solution)/shard_map/ppermute | solution.py:31
  797.3 95.1 %collective-permute-start.9 = (bf16[64,16384]{1,0:T(8,128)(2,1)}, bf16[64,16384]{1,0:T(8,128)(2,1)}, u32[]{:S(2)}, u32[]{:S(2)}) collective-permute-start(bf16[64,16384]{1,0:T(8,128)(2,1)} %get-tuple-element.138), channel_id=1, source_target_pairs={{16,0},{17,1},{18,2},{19,3},{20,4},{21,5},{22,6},{23,7},{24,8},{25... | collective-permute-start | bytes 6291464 | tf_op jit(solution)/shard_map/ppermute | solution.py:31
  (16 other events, 222.4 us)
